TPU v7x, 128 devices: a whole 4x4x4 slice. The times are simulated.
128 devices in a mesh: seq: 16 (over z, x), tp: 8 (over y, core).
Axes of the slice: x: 4, y: 4, z: 4, core: 2. Of those that a mesh axis runs over, the one named last changes fastest.
Arguments:
- tokens: bfloat16 [2048, 6144], P('seq', 'tp'), may hold values from -6 to 6
- router_weight: bfloat16 [6144, 8], P('tp'), may hold values from -0.15625 to 0.15625
- expert_ids: int32 [2048, 2], P('seq'), may hold values from 0 to 7, all different within a row; in each aligned block of 128 rows (0 to 127, 128 to 255, ...) at most 56 rows name the same one
- gate_weight: bfloat16 [16, 6144, 4096], P('seq', None, 'tp'), may hold values from -0.078125 to 0.078125
- up_weight: bfloat16 [16, 6144, 4096], P('seq', None, 'tp'), may hold values from -0.078125 to 0.078125
- down_weight: bfloat16 [16, 4096, 6144], P('seq', 'tp'), may hold values from -0.0625 to 0.0625
Outputs:
- mixed: bfloat16 [2048, 6144], P('seq', 'tp')
Inputs may be any that keep to these rules, and one draw needn't show every extreme that they name: `expert_ids`: each row names 2 different experts. In each aligned block of 128 rows (the tokens of one sequence group) no expert is named more than 56 times, a bound that some block reaches.
All inputs are finite; a program needn't handle non-finite values.
Results may differ from a plain program's by a relative error of at most 0.014.
Values may be sent and summed in bfloat16 or wider, within the bound.
No kernel may reach another device: no remote copies, remote signals or barrier semaphores. Data moves between devices by JAX's collectives and lax.ppermute only.
A program may use at most 128 MiB of HBM per device.

v0:
```python
import jax
import jax.numpy as jnp
from jax import lax
from jax.sharding import PartitionSpec as P

D = 6144
CAP = 56


def sent_to_all(array, axis):
    length = lax.axis_size(axis)
    return lax.all_to_all(
        jnp.broadcast_to(array[None], (length, *array.shape)), axis, 0, 0, tiled=True
    )


def over_copies(array, axis):
    return sent_to_all(array, axis).sum(axis=0)


def slot_numbers(expert_ids, experts):
    flat_ids = expert_ids.reshape(-1)
    onehot = (flat_ids[:, None] == jnp.arange(experts, dtype=jnp.int32)[None, :]).astype(jnp.int32)
    before = jnp.cumsum(onehot, axis=0) - onehot
    return (flat_ids, jnp.sum(before * onehot, axis=1))


def per_device(tokens, router_weight, expert_ids, gate_weight, up_weight, down_weight):
    seq_count = lax.axis_size("seq")
    experts = router_weight.shape[1]
    halves = seq_count // experts
    tok_rows, top_count = expert_ids.shape
    capacity = CAP
    width = D
    gate_slab = gate_weight[0]
    up_slab = up_weight[0]
    down_slab = down_weight[0]
    partial_logits = jnp.dot(tokens, router_weight, preferred_element_type=jnp.float32)
    logits = over_copies(partial_logits, "tp")
    chosen = expert_ids[:, :, None] == jnp.arange(experts, dtype=jnp.int32)[None, None, :]
    picked = jnp.sum(jnp.where(chosen, logits[:, None, :], 0.0), axis=2)
    gates = jax.nn.sigmoid(picked - picked[:, ::-1])
    flat_ids, slots = slot_numbers(expert_ids, experts)
    row_index = jnp.arange(seq_count * capacity, dtype=jnp.int32)
    row_expert = row_index // capacity // halves
    row_slot = row_index % capacity
    matches = (row_expert[:, None] == flat_ids[None, :]) & (row_slot[:, None] == slots[None, :])
    select = jnp.any(matches.reshape(seq_count * capacity, tok_rows, top_count), axis=2).astype(
        jnp.bfloat16
    )
    outgoing = jnp.dot(select, tokens, preferred_element_type=jnp.float32).astype(jnp.bfloat16)
    outgoing = outgoing.reshape(seq_count, capacity, tokens.shape[1])
    received = lax.all_to_all(outgoing, "seq", split_axis=0, concat_axis=0, tiled=True)
    count = received.shape[1]
    piece = lax.all_gather(received, "tp", axis=2, tiled=True)
    piece_rows = piece.reshape(-1, piece.shape[2])
    gate = jnp.dot(piece_rows, gate_slab, preferred_element_type=jnp.float32)
    up = jnp.dot(piece_rows, up_slab, preferred_element_type=jnp.float32)
    hidden = (jax.nn.silu(gate) * up).astype(jnp.bfloat16)
    partial_value = jnp.dot(hidden, down_slab, preferred_element_type=jnp.float32).reshape(
        seq_count, count, width
    )
    reduced = lax.psum_scatter(
        partial_value.astype(jnp.bfloat16), "tp", scatter_dimension=2, tiled=True
    ).astype(jnp.float32)
    returned = lax.all_to_all(
        reduced.astype(jnp.bfloat16), "seq", split_axis=0, concat_axis=0, tiled=True
    ).astype(reduced.dtype)
    columns = returned.shape[2]
    summed = jnp.sum(returned.reshape(experts, halves, capacity, columns), axis=1)
    summed = summed.reshape(experts * capacity, columns)
    gathered = summed[flat_ids * capacity + slots].reshape(tok_rows, top_count, columns)
    mixed = jnp.sum(gathered * gates[:, :, None], axis=1)
    return mixed.astype(jnp.bfloat16)


def solution(mesh):
    in_specs = (
        P("seq", "tp"),
        P("tp", None),
        P("seq", None),
        P("seq", None, "tp"),
        P("seq", None, "tp"),
        P("seq", "tp", None),
    )
    out_specs = P("seq", "tp")
    return jax.shard_map(
        per_device, mesh=mesh, in_specs=in_specs, out_specs=out_specs, check_vma=False
    )
```

profile of v0, /device:TPU:9, one launch (start us, length us, event | category | flops | bytes accessed | tf_op | source)
XLA Modules:
  0.0 233.1 jit_solution(17153037409730043633)
XLA Ops:
  6.5 0.0 copy-start
  6.5 0.0 all-gather.2.cloned.1.call-start
  6.5 0.8 copy.27
  7.4 0.1 eq.78
  7.5 0.1 eq.74
  7.7 0.6 reduce-window.6
  8.3 0.2 slice_reduce_fusion
  8.5 0.1 fusion.8
  8.6 0.1 eq.82
  8.8 0.1 copy.29
  8.8 1.0 and_reduce_fusion
  9.9 0.0 copy-done
  9.9 0.5 convolution_convert_fusion.1
  10.4 27.4 %all_to_all.15 = bf16[16,56,768]{2,1,0:T(8,128)(2,1)} all-to-all(bf16[16,56,768]{2,1,0:T(8,128)(2,1)S(1)} %bitcast.37), channel_id=1, replica_groups=mesh['seq'=16,'tp'=8] {'seq'}, dimensions={0} | all-to-all | bytes 2752512 | tf_op jit(solution)/shard_map/all_to_all | solution.py:53
  37.8 0.0 all-gather.2.cloned.1.call-update
  37.8 0.0 reduce-scatter.2.cloned.1.call-start
  37.8 59.0 %all-gather.2.cloned.1.call-done = bf16[16,56,6144]{2,1,0:T(8,128)(2,1)} async-done(((bf16[16,56,768]{2,1,0:T(8,128)(2,1)}), bf16[16,56,6144]{2,1,0:T(8,128)(2,1)}) %all-gather.2.cloned.1.call-update) | async-done | bytes 11010064 | tf_op jit(solution)/shard_map/all_gather | solution.py:55
  96.9 0.0 copy-start.3
  96.9 10.6 %fusion.3 = f32[896,512]{1,0:T(8,128)S(1)} fusion(bf16[896,6144]{1,0:T(8,128)(2,1)} %bitcast.40, bf16[1,6144,512]{2,1,0:T(8,128)(2,1)} %param.9), kind=kOutput, calls=%fused_computation.5 | convolution fusion | flops 5637144576 | bytes 19136512 | tf_op jit(solution)/shard_map/dot_general | solution.py:57
  107.4 0.0 copy-done.3
  107.5 8.0 %multiply_convert_fusion = bf16[896,512]{1,0:T(8,128)(2,1)S(1)} fusion(f32[896,512]{1,0:T(8,128)S(1)} %fusion.3, bf16[896,6144]{1,0:T(8,128)(2,1)S(1)} %bitcast.41, bf16[1,6144,512]{2,1,0:T(8,128)(2,1)} %param.10), kind=kOutput, calls=%fused_computation.8 | convolution fusion | flops 5639897088 | bytes 20054016 | tf_op jit(solution)/shard_map/dot_general | solution.py:58
  115.5 11.3 %convolution_convert_fusion = bf16[16,56,6144]{2,1,0:T(8,128)(2,1)} fusion(bf16[16,56,512]{2,1,0:T(8,128)(2,1)S(1)} %bitcast.42, bf16[1,512,6144]{2,1,0:T(8,128)(2,1)} %param.11), kind=kOutput, calls=%fused_computation.1 | convolution fusion | flops 5642649600 | bytes 18219008 | tf_op jit(solution)/shard_map/dot_general | solution.py:60
  126.8 0.0 copy-start.2
  126.8 0.0 copy-start.1
  126.8 0.0 reduce-scatter.2.cloned.1.call-update
  126.9 0.7 copy-done.2
  127.5 0.1 fusion.19
  127.7 7.9 %all_to_all.16 = f32[8,128,8]{1,2,0:T(8,128)S(1)} all-to-all(f32[8,128,8]{1,2,0:T(8,128)S(1)} %broadcast_in_dim.10), channel_id=1, replica_groups=mesh['seq'=16,'tp'=8] {'tp'}, dimensions={0} | all-to-all | bytes 65536 | tf_op jit(solution)/shard_map/all_to_all | solution.py:12
  135.6 56.1 %reduce-scatter.2.cloned.1.call-done = bf16[16,56,768]{2,1,0:T(8,128)(2,1)} async-done(((bf16[16,56,6144]{2,1,0:T(8,128)(2,1)}), bf16[16,56,768]{2,1,0:T(8,128)(2,1)}) %reduce-scatter.2.cloned.1.call-update) | async-done | bytes 1376272 | tf_op jit(solution)/shard_map/reduce_scatter | solution.py:63
  191.7 6.7 %all-to-all-start.1 = ((bf16[16,56,768]{2,1,0:T(8,128)(2,1)}), bf16[16,56,768]{2,1,0:T(8,128)(2,1)S(1)}, u32[]{:S(2)}, u32[]{:S(2)}) async-start(bf16[16,56,768]{2,1,0:T(8,128)(2,1)} %reduce-scatter.2.cloned.1.call-done), calls=%async_computation.2 | async-start | bytes 2752512 | tf_op jit(solution)/shard_map/all_to_all | solution.py:66
  198.3 0.0 copy-done.1
  198.4 0.1 copy.30
  198.5 0.1 mul.39
  198.7 0.1 copy.31
  198.8 24.0 %all-to-all-done.1 = bf16[16,56,768]{2,1,0:T(8,128)(2,1)S(1)} async-done(((bf16[16,56,768]{2,1,0:T(8,128)(2,1)}), bf16[16,56,768]{2,1,0:T(8,128)(2,1)S(1)}, u32[]{:S(2)}, u32[]{:S(2)}) %all-to-all-start.1) | async-done | bytes 1376288 | tf_op jit(solution)/shard_map/all_to_all | solution.py:66
  222.8 0.2 convert_reduce_fusion
  223.0 1.1 gather_fusion
  224.1 0.5 reshape.133
  224.6 1.7 multiply_reduce_fusion
  (12 shorter events, 0.2 us)
Async XLA Ops:
  6.5 3.3 %copy-start = (bf16[128,768]{1,0:T(8,128)(2,1)S(1)}, bf16[128,768]{1,0:T(8,128)(2,1)}, u32[]{:S(2)}) copy-start(bf16[128,768]{1,0:T(8,128)(2,1)} %param.6) | copy-start | bytes 589828
  6.5 90.3 %all-gather.2.cloned.1.call-start = ((), (), s32[]{:S(2)}) async-start(), calls=%async_computation.4 | async-start | bytes 12386304 | tf_op jit(solution)/shard_map/all_gather | solution.py:55
  37.8 153.9 %reduce-scatter.2.cloned.1.call-start = ((), (), s32[]{:S(2)}) async-start(), calls=%async_computation.5 | async-start | bytes 12386304 | tf_op jit(solution)/shard_map/reduce_scatter | solution.py:63
  96.9 10.6 %copy-start.3 = (bf16[16,56,6144]{2,1,0:T(8,128)(2,1)S(1)}, bf16[16,56,6144]{2,1,0:T(8,128)(2,1)}, u32[]{:S(2)}) copy-start(bf16[16,56,6144]{2,1,0:T(8,128)(2,1)} %all-gather.2.cloned.1.call-done) | copy-start | bytes 33030148
  126.8 0.7 copy-start.2
  126.8 71.5 %copy-start.1 = (s32[128,2]{0,1:T(2,128)S(1)}, s32[128,2]{0,1:T(2,128)}, u32[]{:S(2)}) copy-start(s32[128,2]{0,1:T(2,128)} %param.8) | copy-start | bytes 3076
  191.7 31.1 %all-to-all-start.1 = ((bf16[16,56,768]{2,1,0:T(8,128)(2,1)}), bf16[16,56,768]{2,1,0:T(8,128)(2,1)S(1)}, u32[]{:S(2)}, u32[]{:S(2)}) async-start(bf16[16,56,768]{2,1,0:T(8,128)(2,1)} %reduce-scatter.2.cloned.1.call-done), calls=%async_computation.2 | async-start | bytes 2752512 | tf_op jit(solution)/shard_map/all_to_all | solution.py:66
Sparse Core Ops, SparseCore 0:
  37.9 58.9 all-gather.1
  127.0 64.6 reduce-scatter.1
where the time goes:
time: 233 us
  waiting for transfers between devices  139 us (60%)
  blocking collectives  35.3 us (15%)
  matrix products  30.6 us (13%)
  between operations  13.6 us (6%)
  starting transfers between devices  6.71 us (3%)
  local copies, waits for them, and re-layouts  4.17 us (2%)
  other arithmetic  3.74 us (2%)
    all_gather x1, waiting for transfers between devices, per_device(): piece = lax.all_gather(received, 'tp', axis=2, tiled=True)  59 us
    reduce_scatter x1, waiting for transfers between devices, per_device(): lax.psum_scatter(partial_value.astype(jnp.bfloat16), 'tp', scatter_dimens...  56.1 us
    all_to_all x1, blocking collectives, per_device(): lax.all_to_all(outgoing, 'seq', split_axis=0, concat_axis=0, tiled=True)  27.4 us
    all_to_all x1, waiting for transfers between devices, per_device(): lax.all_to_all(reduced.astype(jnp.bfloat16), 'seq', split_axis=0, concat_...  24 us
    dot_general x1, matrix products, per_device(): jnp.dot(hidden, down_slab, preferred_element_type=jnp.float32)  11.3 us
    dot_general x1, matrix products, per_device(): gate = jnp.dot(piece_rows, gate_slab, preferred_element_type=jnp.float32)  10.6 us
    dot_general x1, matrix products, per_device(): up = jnp.dot(piece_rows, up_slab, preferred_element_type=jnp.float32)  8.03 us
    all_to_all x1, blocking collectives, sent_to_all(): lax.all_to_all(jnp.broadcast_to(array[None], (length, *array.shape)), axi...  7.9 us
  transfers between devices with their start and end apart: 3, of which 3 were waited for; matrix products, arithmetic and copies ran while one was open for 0% of the time, Pallas kernels for 0%

commit v1 on v0

--- a/solution.py
+++ b/solution.py
@@ -52,7 +52,11 @@
     outgoing = outgoing.reshape(seq_count, capacity, tokens.shape[1])
     received = lax.all_to_all(outgoing, "seq", split_axis=0, concat_axis=0, tiled=True)
     count = received.shape[1]
-    piece = lax.all_gather(received, "tp", axis=2, tiled=True)
+    size = lax.axis_size("tp")
+    repeats = [size if d == 2 else 1 for d in range(received.ndim)]
+    piece = lax.all_to_all(
+        jnp.tile(received, repeats), "tp", split_axis=2, concat_axis=2, tiled=True
+    )
     piece_rows = piece.reshape(-1, piece.shape[2])
     gate = jnp.dot(piece_rows, gate_slab, preferred_element_type=jnp.float32)
     up = jnp.dot(piece_rows, up_slab, preferred_element_type=jnp.float32)

time: 233 us -> 433 us (1.86)
  local copies, waits for them, and re-layouts: 4.17 us -> 138 us
  blocking collectives: 35.3 us -> 165 us
  waiting for transfers between devices: 139 us -> 76.3 us
    all_to_all x0 -> x1, blocking collectives: none -> 130 us  [per_device(): lax.all_to_all(jnp.tile(received, repeats), 'tp', split_axis=2, concat_ax...]
    unnamed x9 -> x15, local copies, waits for them, and re-layouts: 1.52 us -> 93.9 us
    all_gather x1 -> x0, waiting for transfers between devices: 59 us -> none  [per_device(): piece = lax.all_gather(received, 'tp', axis=2, tiled=True)]
    all_to_all x0 -> x2, local copies, waits for them, and re-layouts: none -> 30.7 us  [the longest x1 26.8 us: per_device(): lax.all_to_all(jnp.tile(received, repeats), 'tp', split_axis=2, concat_ax...]
    another operation x1 -> x2, local copies, waits for them, and re-layouts: 0.01 us -> 10.4 us  [the longest x1 10.4 us: per_device(): jnp.tile(received, repeats)]
  transfers between devices with their start and end apart: 3 -> 2, of which waited for: 3 -> 2; matrix products, arithmetic and copies ran while one was open for 0% -> 0% of each run, Pallas kernels for 0% -> 0%
where the time goes in v1:
time: 433 us; the launch traced here: 432 us
  blocking collectives  165 us (38%)
  local copies, waits for them, and re-layouts  138 us (32%)
  waiting for transfers between devices  76.3 us (18%)
  matrix products  28.8 us (7%)
  between operations  13.6 us (3%)
  starting transfers between devices  6.41 us (1%)
    all_to_all x1, blocking collectives, per_device(): lax.all_to_all(jnp.tile(received, repeats), 'tp', split_axis=2, concat_ax...  130 us
    unnamed x15, local copies, waits for them, and re-layouts  93.9 us
    reduce_scatter x1, waiting for transfers between devices, per_device(): lax.psum_scatter(partial_value.astype(jnp.bfloat16), 'tp', scatter_dimens...  52.3 us
    all_to_all x1, blocking collectives, per_device(): lax.all_to_all(outgoing, 'seq', split_axis=0, concat_axis=0, tiled=True)  27.4 us
    all_to_all x1, local copies, waits for them, and re-layouts, per_device(): lax.all_to_all(jnp.tile(received, repeats), 'tp', split_axis=2, concat_ax...  26.8 us
    all_to_all x1, waiting for transfers between devices, per_device(): lax.all_to_all(reduced.astype(jnp.bfloat16), 'seq', split_axis=0, concat_...  24 us
    dot_general x1, matrix products, per_device(): jnp.dot(hidden, down_slab, preferred_element_type=jnp.float32)  11.6 us
    dot_general x1, matrix products, per_device(): gate = jnp.dot(piece_rows, gate_slab, preferred_element_type=jnp.float32)  10.6 us
  transfers between devices with their start and end apart: 2, of which 2 were waited for; matrix products, arithmetic and copies ran while one was open for 0% of the time, Pallas kernels for 0%

profile of v1, /device:TPU:9, one launch (start us, length us, event | category | flops | bytes accessed | tf_op | source)
XLA Modules:
  0.0 431.6 jit_solution(12077083435008833767)
XLA Ops:
  6.5 0.0 copy-start
  6.5 0.0 reduce-scatter.2.cloned.1.call-start
  6.5 0.8 copy.37
  7.4 0.1 eq.78
  7.5 0.1 eq.74
  7.7 0.6 reduce-window.6
  8.3 0.2 slice_reduce_fusion
  8.5 0.1 fusion.8
  8.6 0.1 eq.82
  8.8 0.1 copy.39
  8.8 1.0 and_reduce_fusion
  9.9 0.0 copy-done
  9.9 0.5 convolution_convert_fusion.1
  10.4 27.4 %all_to_all.20 = bf16[16,56,768]{2,1,0:T(8,128)(2,1)} all-to-all(bf16[16,56,768]{2,1,0:T(8,128)(2,1)S(1)} %bitcast.44), channel_id=1, replica_groups=mesh['seq'=16,'tp'=8] {'seq'}, dimensions={0} | all-to-all | bytes 2752512 | tf_op jit(solution)/shard_map/all_to_all | solution.py:53
  37.8 4.0 copy.40
  41.7 10.4 %tile.4 = bf16[16,56,8,768]{1,0,3,2:T(8,128)(2,1)} broadcast(bf16[16,56,768]{1,0,2:T(8,128)(2,1)S(1)} %copy.40), dimensions={0,1,3} | broadcast | bytes 12386304 | tf_op jit(solution)/shard_map/tile | solution.py:58
  52.1 47.1 %reshape.150 = bf16[8,2,344064]{2,1,0:T(2,128)(2,1)} reshape(bf16[6144,16,56]{2,1,0:T(8,128)(2,1)} %bitcast.39) | data formatting | bytes 22020096
  99.2 130.1 %all_to_all.21 = bf16[8,2,344064]{2,1,0:T(2,128)(2,1)} all-to-all(bf16[8,2,344064]{2,1,0:T(2,128)(2,1)} %reshape.150), channel_id=1, replica_groups=mesh['seq'=16,'tp'=8] {'tp'}, dimensions={0} | all-to-all | bytes 22020096 | tf_op jit(solution)/shard_map/all_to_all | solution.py:57
  229.3 45.3 %reshape.151 = bf16[6144,16,56]{2,1,0:T(8,128)(2,1)} reshape(bf16[8,2,344064]{2,1,0:T(2,128)(2,1)} %all_to_all.21) | data formatting | bytes 22020096
  274.6 0.0 slice-start
  274.6 26.8 %copy.41 = bf16[16,56,6144]{2,1,0:T(8,128)(2,1)} copy(bf16[16,56,6144]{1,0,2:T(8,128)(2,1)} %bitcast.40) | data formatting | bytes 22020096 | tf_op jit(solution)/shard_map/all_to_all | solution.py:57
  301.4 0.0 copy-start.1
  301.4 0.0 slice-start.1
  301.4 10.6 %fusion.3 = f32[896,512]{1,0:T(8,128)S(1)} fusion(bf16[896,6144]{1,0:T(8,128)(2,1)} %bitcast.42, bf16[1,6144,512]{2,1,0:T(8,128)(2,1)} %param.9), kind=kOutput, calls=%fused_computation.5 | convolution fusion | flops 5637144576 | bytes 19136512 | tf_op jit(solution)/shard_map/dot_general | solution.py:61
  312.0 0.0 slice-done
  312.0 0.0 copy-done.1
  312.0 0.0 slice-done.1
  312.0 6.0 %multiply_convert_fusion = bf16[896,512]{1,0:T(8,128)(2,1)S(1)} fusion(f32[896,512]{1,0:T(8,128)S(1)} %fusion.3, bf16[896,6144]{1,0:T(8,128)(2,1)S(1)} %bitcast.43, bf16[1,6144,512]{2,1,0:T(8,128)(2,1)S(1)} %bitcast.48), kind=kOutput, calls=%fused_computation.8 | convolution fusion | flops 5639897088 | bytes 20054016 | tf_op jit(solution)/shard_map/dot_general | solution.py:62
  318.1 11.6 %convolution_convert_fusion = bf16[16,56,6144]{2,1,0:T(8,128)(2,1)} fusion(bf16[16,56,512]{2,1,0:T(8,128)(2,1)S(1)} %bitcast.49, bf16[1,512,6144]{2,1,0:T(8,128)(2,1)} %param.11), kind=kOutput, calls=%fused_computation.1 | convolution fusion | flops 5642649600 | bytes 18219008 | tf_op jit(solution)/shard_map/dot_general | solution.py:64
  329.6 0.0 copy-start.3
  329.6 0.0 copy-start.2
  329.6 0.0 reduce-scatter.2.cloned.1.call-update
  329.7 0.7 copy-done.3
  330.3 0.1 fusion.19
  330.5 7.6 %all_to_all.22 = f32[8,128,8]{1,2,0:T(8,128)S(1)} all-to-all(f32[8,128,8]{1,2,0:T(8,128)S(1)} %broadcast_in_dim.10), channel_id=1, replica_groups=mesh['seq'=16,'tp'=8] {'tp'}, dimensions={0} | all-to-all | bytes 65536 | tf_op jit(solution)/shard_map/all_to_all | solution.py:12
  338.0 52.3 %reduce-scatter.2.cloned.1.call-done = bf16[16,56,768]{2,1,0:T(8,128)(2,1)} async-done(((bf16[16,56,6144]{2,1,0:T(8,128)(2,1)}), bf16[16,56,768]{2,1,0:T(8,128)(2,1)}) %reduce-scatter.2.cloned.1.call-update) | async-done | bytes 1376272 | tf_op jit(solution)/shard_map/reduce_scatter | solution.py:67
  390.4 6.4 %all-to-all-start.2 = ((bf16[16,56,768]{2,1,0:T(8,128)(2,1)}), bf16[16,56,768]{2,1,0:T(8,128)(2,1)S(1)}, u32[]{:S(2)}, u32[]{:S(2)}) async-start(bf16[16,56,768]{2,1,0:T(8,128)(2,1)} %reduce-scatter.2.cloned.1.call-done), calls=%async_computation.3 | async-start | bytes 2752512 | tf_op jit(solution)/shard_map/all_to_all | solution.py:70
  396.8 0.0 copy-done.2
  396.8 0.1 copy.42
  396.9 0.1 mul.39
  397.2 0.1 copy.43
  397.3 24.0 %all-to-all-done.2 = bf16[16,56,768]{2,1,0:T(8,128)(2,1)S(1)} async-done(((bf16[16,56,768]{2,1,0:T(8,128)(2,1)}), bf16[16,56,768]{2,1,0:T(8,128)(2,1)S(1)}, u32[]{:S(2)}, u32[]{:S(2)}) %all-to-all-start.2) | async-done | bytes 1376288 | tf_op jit(solution)/shard_map/all_to_all | solution.py:70
  421.3 0.2 convert_reduce_fusion
  421.5 1.1 gather_fusion
  422.6 0.5 reshape.137
  423.1 1.7 multiply_reduce_fusion
  (13 shorter events, 0.2 us)
Async XLA Ops:
  6.5 3.3 copy-start
  6.5 383.8 %reduce-scatter.2.cloned.1.call-start = ((), (), s32[]{:S(2)}) async-start(), calls=%async_computation.5 | async-start | bytes 12386304 | tf_op jit(solution)/shard_map/reduce_scatter | solution.py:67
  274.6 37.3 %slice-start = ((s8[6291456]{0:T(1024)(128)(4,1)}), s8[2097152]{0:T(1024)(128)(4,1)S(1)}, s32[]{:S(2)}) async-start(s8[6291456]{0:T(1024)(128)(4,1)} %bitcast.47), calls=%async_computation.6 | async-start | bytes 4194304
  301.4 10.6 %copy-start.1 = (bf16[16,56,6144]{2,1,0:T(8,128)(2,1)S(1)}, bf16[16,56,6144]{2,1,0:T(8,128)(2,1)}, u32[]{:S(2)}) copy-start(bf16[16,56,6144]{2,1,0:T(8,128)(2,1)} %copy.41) | copy-start | bytes 33030148
  301.4 10.6 %slice-start.1 = ((s8[6291456]{0:T(1024)(128)(4,1)}), s8[4194304]{0:T(1024)(128)(4,1)S(1)}, s32[]{:S(2)}) async-start(s8[6291456]{0:T(1024)(128)(4,1)} %bitcast.47), calls=%async_computation.7 | async-start | bytes 8388608
  329.6 0.7 copy-start.3
  329.6 67.2 %copy-start.2 = (s32[128,2]{0,1:T(2,128)S(1)}, s32[128,2]{0,1:T(2,128)}, u32[]{:S(2)}) copy-start(s32[128,2]{0,1:T(2,128)} %param.8) | copy-start | bytes 3076
  390.4 30.9 %all-to-all-start.2 = ((bf16[16,56,768]{2,1,0:T(8,128)(2,1)}), bf16[16,56,768]{2,1,0:T(8,128)(2,1)S(1)}, u32[]{:S(2)}, u32[]{:S(2)}) async-start(bf16[16,56,768]{2,1,0:T(8,128)(2,1)} %reduce-scatter.2.cloned.1.call-done), calls=%async_computation.3 | async-start | bytes 2752512 | tf_op jit(solution)/shard_map/all_to_all | solution.py:70
Sparse Core Ops, SparseCore 0:
  329.8 60.5 reduce-scatter.1
